TPU v7x, 32 devices: a whole 2x2x4 slice. The times are simulated.
32 devices in a mesh: heads: 4 (over y, core), tokens: 4 (over z), cols: 2 (over x).
Axes of the slice: x: 2, y: 2, z: 4, core: 2. Of those that a mesh axis runs over, the one named last changes fastest.
Arguments:
- query_in: bfloat16 [2048, 8192], P('tokens', ('heads', 'cols')), may hold values from -24 to 24
- key_in: bfloat16 [2048, 8192], P('tokens', ('heads', 'cols')), may hold values from -24 to 24
- value_in: bfloat16 [2048, 8192], P('tokens', ('heads', 'cols')), may hold values from -6 to 6
- out_grads: bfloat16 [2048, 8192], P('tokens', ('heads', 'cols')), may hold values from -6 to 6
- doc_starts: int32 [6], replicated, may hold values from 0 to 2047, as said below
Outputs:
- input_factor: float32 [8192, 8192], P('heads', ('tokens', 'cols'))
- grad_factor: float32 [8192, 8192], P('heads', ('tokens', 'cols'))
Inputs may be any that keep to these rules, and one draw needn't show every extreme that they name: Strictly increasing with the first entry 0; document d runs from doc_starts[d] to the next start (the last one to 2048) - 1. One document holds (4 // 2 + 1) * 512 tokens.
All inputs are finite; a program needn't handle non-finite values.
Results may differ from a plain program's by a relative error of at most 0.0041.
Values may be sent and summed in bfloat16 or wider, within the bound.
A program may use at most 128 MiB of HBM per device.

v0:
```python
import math
import jax
import jax.numpy as jnp
from jax import lax
from jax.sharding import PartitionSpec as P

HEAD_DIM = 128
MASK_FLOOR = -1e30


def spread(value, axis, source):
    kept = jnp.where(lax.axis_index(axis) == source, value, 0).astype(value.dtype)
    return lax.psum(kept, axis)


def document_ids(positions, doc_starts):
    return jnp.sum((positions[:, None] >= doc_starts[None, :]).astype(jnp.int32), axis=1) - 1


def pair_scores(query_rows, key_rows, query_pos, key_pos, doc_starts):
    head_count = query_rows.shape[1] // HEAD_DIM
    query_heads = query_rows.reshape(query_rows.shape[0], head_count, HEAD_DIM)
    key_heads = key_rows.reshape(key_rows.shape[0], head_count, HEAD_DIM)
    scores = jnp.einsum(
        "qhd,khd->hqk", query_heads, key_heads, preferred_element_type=jnp.float32
    ) * (1.0 / math.sqrt(HEAD_DIM))
    query_docs = document_ids(query_pos, doc_starts)
    key_docs = document_ids(key_pos, doc_starts)
    allowed = query_docs[:, None] == key_docs[None, :]
    return (scores, allowed[None, :, :])


def on_device(query_in, key_in, value_in, out_grads, doc_starts):
    tok_dev, row_width = query_in.shape
    head_count = row_width // HEAD_DIM
    first_pos = lax.axis_index("tokens") * tok_dev
    query_pos = first_pos + jnp.arange(tok_dev, dtype=jnp.int32)
    keys_all, values_all = (
        lax.all_gather(key_in, "tokens", axis=0, tiled=True),
        lax.all_gather(value_in, "tokens", axis=0, tiled=True),
    )
    all_tokens = keys_all.shape[0]
    key_span = min(512, all_tokens)
    block_ids = jnp.arange(all_tokens // key_span, dtype=jnp.int32)

    def block_scores(block_id):
        key_begin = block_id * key_span
        key_rows = lax.dynamic_slice_in_dim(keys_all, key_begin, key_span, 0)
        key_pos = key_begin + jnp.arange(key_span, dtype=jnp.int32)
        scores, allowed = pair_scores(query_in, key_rows, query_pos, key_pos, doc_starts)
        return (key_begin, scores, allowed)

    def gated(block_id, update, running):
        key_begin = block_id * key_span
        return update(running)

    def stats_step(running, block_id):

        def update(state):
            row_peak, row_mass = state
            key_begin, scores, allowed = block_scores(block_id)
            masked = jnp.where(allowed, scores, MASK_FLOOR)
            new_peak = jnp.maximum(row_peak, jnp.max(masked, axis=2))
            new_mass = row_mass * jnp.exp(row_peak - new_peak) + jnp.sum(
                jnp.where(allowed, jnp.exp(masked - new_peak[:, :, None]), 0.0), axis=2
            )
            return (new_peak, new_mass)

        return (gated(block_id, update, running), None)

    initial = (
        jnp.full((head_count, tok_dev), MASK_FLOOR, jnp.float32),
        jnp.zeros((head_count, tok_dev), jnp.float32),
    )
    (row_peak, row_mass), _ = lax.scan(stats_step, initial, block_ids)
    log_total = row_peak + jnp.log(row_mass)

    def value_step(running, block_id):

        def update(state):
            weighted, partials = state
            key_begin, scores, allowed = block_scores(block_id)
            weights = jnp.where(allowed, jnp.exp(scores - log_total[:, :, None]), 0.0).astype(
                jnp.bfloat16
            )
            value_rows = lax.dynamic_slice_in_dim(values_all, key_begin, key_span, 0).reshape(
                key_span, head_count, HEAD_DIM
            )
            weighted = weighted + jnp.einsum(
                "hqk,khd->qhd", weights, value_rows, preferred_element_type=jnp.float32
            )
            return (weighted, partials)

        return (gated(block_id, update, running), None)

    partial_rows = 8
    value_init = (
        jnp.zeros((tok_dev, head_count, HEAD_DIM), jnp.float32),
        jnp.zeros((partial_rows, row_width), jnp.float32),
    )
    (weighted, partials), _ = lax.scan(value_step, value_init, block_ids)
    attended = weighted.reshape(tok_dev, row_width).astype(jnp.bfloat16)
    stats_all = lax.all_gather(log_total.T, "tokens", axis=0, tiled=True)
    query_rows = lax.all_gather(query_in, "tokens", axis=0, tiled=True)
    grad_rows = lax.all_gather(out_grads, "tokens", axis=0, tiled=True)
    piece_rows = query_rows.shape[0]
    piece_pos = jnp.arange(piece_rows, dtype=jnp.int32)

    def update(grad_sum):
        scores, allowed = pair_scores(query_rows, key_in, piece_pos, query_pos, doc_starts)
        weights = jnp.where(allowed, jnp.exp(scores - stats_all.T[:, :, None]), 0.0).astype(
            jnp.bfloat16
        )
        piece_grads = grad_rows.reshape(piece_rows, head_count, HEAD_DIM)
        return jnp.einsum("hqk,qhd->khd", weights, piece_grads, preferred_element_type=jnp.float32)

    summed = update(jnp.zeros((tok_dev, head_count, HEAD_DIM), jnp.float32))
    value_grads = summed.reshape(tok_dev, row_width).astype(jnp.bfloat16)
    token_shards = lax.axis_size("tokens")
    col_shards = lax.axis_size("cols")
    rows_attended, rows_grads = (
        lax.all_gather(attended[None], ("tokens", "cols"), axis=0, tiled=True),
        lax.all_gather(value_grads[None], ("tokens", "cols"), axis=0, tiled=True),
    )
    rows_attended = rows_attended.reshape(token_shards, col_shards, tok_dev, row_width)
    rows_grads = rows_grads.reshape(token_shards, col_shards, tok_dev, row_width)
    own_attended = lax.dynamic_index_in_dim(
        rows_attended, lax.axis_index("cols"), 1, keepdims=False
    )
    own_grads = lax.dynamic_index_in_dim(rows_grads, lax.axis_index("cols"), 1, keepdims=False)
    cols_attended, cols_grads = (
        spread(own_attended, "heads", lax.axis_index("tokens")),
        spread(own_grads, "heads", lax.axis_index("tokens")),
    )
    input_factor = jnp.einsum(
        "acnf,ang->cfg", rows_attended, cols_attended, preferred_element_type=jnp.float32
    )
    grad_factor = jnp.einsum(
        "acnf,ang->cfg", rows_grads, cols_grads, preferred_element_type=jnp.float32
    )
    input_factor = input_factor.reshape(col_shards * row_width, row_width) / all_tokens
    grad_factor = grad_factor.reshape(col_shards * row_width, row_width) / all_tokens
    return (input_factor, grad_factor)


def solution(mesh):
    in_specs = (
        P("tokens", ("heads", "cols")),
        P("tokens", ("heads", "cols")),
        P("tokens", ("heads", "cols")),
        P("tokens", ("heads", "cols")),
        P(),
    )
    out_specs = (P("heads", ("tokens", "cols")), P("heads", ("tokens", "cols")))
    return jax.shard_map(
        on_device, mesh=mesh, in_specs=in_specs, out_specs=out_specs, check_vma=False
    )
```

profile of v0, /device:TPU:0, one launch (start us, length us, event | category | flops | bytes accessed | tf_op | source)
XLA Modules:
  0.0 775.8 jit_solution(3249628128545039161)
XLA Ops:
  7.2 2.4 copy.58
  9.7 2.3 copy.57
  12.8 2.3 copy.62
  15.1 78.1 %all-gather.9.cloned.1.call-done = bf16[2048,1024]{0,1:T(8,128)(2,1)} async-done(((bf16[512,1024]{0,1:T(8,128)(2,1)}), bf16[2048,1024]{0,1:T(8,128)(2,1)}) %all-gather.9.cloned.1.call-update) | async-done | bytes 4194320 | tf_op jit(solution)/shard_map/all_gather | solution.py:39
  93.2 27.0 %while.30 = (s32[]{:T(128)}, f32[8,512]{1,0:T(8,128)S(1)}, f32[8,512]{1,0:T(8,128)S(1)}, s32[6]{0:T(128)S(1)}, s32[4]{0:T(128)S(1)}, /*index=5*/bf16[2048,1024]{...) while((s32[]{:T(128)}, f32[8,512]{1,0:T(8,128)S(1)}, ...), condition=%wide.region_5.6_spmd.clone, body=%wide.region_0.5_spmd.clone.sunk | while | flops 553950208 | bytes 21995748 | solution.py:75
  96.1 1.7 fusion.59
  97.9 2.0 select_reduce_fusion.2
  104.7 2.0 select_reduce_fusion.2
  111.4 2.0 select_reduce_fusion.2
  118.2 2.0 select_reduce_fusion.2
  120.3 54.3 %all-gather.7.cloned.1.call-done = bf16[2048,1024]{0,1:T(8,128)(2,1)} async-done(((bf16[512,1024]{0,1:T(8,128)(2,1)}), bf16[2048,1024]{0,1:T(8,128)(2,1)}) %all-gather.7.cloned.1.call-update) | async-done | bytes 4194320 | tf_op jit(solution)/shard_map/all_gather | solution.py:40
  174.6 34.2 %while.31 = (s32[]{:T(128)}, f32[512,8,128]{0,2,1:T(8,128)}, s32[4]{0:T(128)S(1)}, bf16[2048,1024]{0,1:T(8,128)(2,1)}, s32[6]{0:T(128)S(1)}, /*index=5*/bf16[204...) while((s32[]{:T(128)}, f32[512,8,128]{0,2,1:T(8,128)}, ...), condition=%wide.region_9.10_spmd.clone, body=%wide.region_6.9_spmd.clone.sunk | while | flops 1083460608 | bytes 12099821 | solution.py:101
  177.9 4.0 bitcast_add_fusion.2
  183.5 1.9 constant_dynamic-slice_fusion.6
  185.4 5.6 bitcast_add_fusion.2
  194.3 5.6 bitcast_add_fusion.2
  203.2 5.6 bitcast_add_fusion.2
  208.8 1.8 convert_element_type.76
  213.0 42.4 %all-gather.15.cloned.1.call-done = bf16[2048,1024]{1,0:T(8,128)(2,1)} async-done(((bf16[512,1024]{1,0:T(8,128)(2,1)}), bf16[2048,1024]{1,0:T(8,128)(2,1)}) %all-gather.15.cloned.1.call-update) | async-done | bytes 4194320 | tf_op jit(solution)/shard_map/all_gather | solution.py:105
  255.5 6.4 copy.65
  261.9 15.2 %all_gather.25 = f32[2048,8]{0,1:T(8,128)S(1)} all-gather(f32[512,8]{0,1:T(8,128)S(1)} %bitcast.132), channel_id=1, replica_groups=mesh['heads'=4,'tokens'=4,'cols'=2] {'tokens'}, dimensions={0}, use_global_device_ids=true | all-gather | bytes 81920 | tf_op jit(solution)/shard_map/all_gather | solution.py:103
  277.1 59.8 %all-gather.13.cloned.1.call-done = bf16[2048,1024]{0,1:T(8,128)(2,1)} async-done(((bf16[512,1024]{0,1:T(8,128)(2,1)}), bf16[2048,1024]{0,1:T(8,128)(2,1)}) %all-gather.13.cloned.1.call-update) | async-done | bytes 4194320 | tf_op jit(solution)/shard_map/all_gather | solution.py:104
  336.9 14.4 %fusion.29 = bf16[8,512,128]{1,2,0:T(8,128)(2,1)S(1)} fusion(bf16[2048,8,128]{0,2,1:T(8,128)(2,1)} %bitcast.130, bf16[2048,8,128]{0,2,1:T(8,128)(2,1)} %bitcast.134, f32[8,2048]{1,0:T(8,128)S(1)} %bitcast.133, pred[2048,512]{1,0:T(8,128)(4,1)S(1)} %broadcast_compare_fusion.2, bf16[512,1024]{1,0:T(8,128)(2,1)S(1)} %copy-done.2), kind=kOutput, calls=%fused_computation.50 | convolution fusion | flops 4329046016 | bytes 11599872 | tf_op jit(solution)/shard_map/hqk,qhd->khd/dot_general | solution.py:115
  353.0 109.4 %all-gather.11.cloned.1.call-done = bf16[8,512,1024]{2,1,0:T(8,128)(2,1)} async-done(((bf16[1,512,1024]{2,1,0:T(8,128)(2,1)}), bf16[8,512,1024]{2,1,0:T(8,128)(2,1)}) %all-gather.11.cloned.1.call-update) | async-done | bytes 8388624 | tf_op jit(solution)/shard_map/all_gather | solution.py:122
  462.4 4.5 fusion.27
  466.9 120.8 %all-gather.17.cloned.1.call-done = bf16[8,512,1024]{2,1,0:T(8,128)(2,1)} async-done(((bf16[1,512,1024]{2,1,0:T(8,128)(2,1)}), bf16[8,512,1024]{2,1,0:T(8,128)(2,1)}) %all-gather.17.cloned.1.call-update) | async-done | bytes 8388624 | tf_op jit(solution)/shard_map/all_gather | solution.py:123
  587.6 4.4 fusion.26
  592.1 11.5 %copy.60 = bf16[2,1024,4,512]{3,1,0,2:T(8,128)(2,1)} copy(bf16[2,1024,4,512]{1,3,0,2:T(8,128)(2,1)} %bitcast.124) | data formatting | bytes 16777216 | tf_op jit(solution)/shard_map/acnf,ang->cfg/dot_general | solution.py:135
  603.6 11.5 %copy.67 = bf16[2,1024,4,512]{3,1,0,2:T(8,128)(2,1)} copy(bf16[2,1024,4,512]{1,3,0,2:T(8,128)(2,1)} %bitcast.126) | data formatting | bytes 16777216 | tf_op jit(solution)/shard_map/acnf,ang->cfg/dot_general | solution.py:138
  615.1 128.2 %all-reduce.3.cloned.1.call-done = (bf16[4,512,1024]{2,1,0:T(8,128)(2,1)}, bf16[4,512,1024]{2,1,0:T(8,128)(2,1)}) async-done(((bf16[4,512,1024]{2,1,0:T(8,128)(2,1)}, bf16[4,512,1024]{2,1,0:T(8,128)(2,1)}), (bf16[4,512,1024]{2,1,0:T(8,128)(2,1)}, bf16[4,512,1024]{2,1,0:T(8,128)(2,1)})) %all-reduce.3.cloned.1.call-update) | async-done | bytes 8388624 | tf_op jit(solution)/shard_map/psum | solution.py:13
  743.3 14.6 %bitcast_multiply_fusion.1 = f32[2048,1024]{1,0:T(8,128)} fusion(bf16[2048,4,512]{2,0,1:T(8,128)(2,1)} %bitcast.128, bf16[4,512,1024]{2,1,0:T(8,128)(2,1)} %get-tuple-element.383), kind=kOutput, calls=%fused_computation.43 | convolution fusion | flops 8592031744 | bytes 20971520 | tf_op jit(solution)/shard_map/acnf,ang->cfg/dot_general | solution.py:135
  757.9 11.0 %bitcast_multiply_fusion = f32[2048,1024]{1,0:T(8,128)} fusion(bf16[2048,4,512]{2,0,1:T(8,128)(2,1)S(1)} %bitcast.127, bf16[4,512,1024]{2,1,0:T(8,128)(2,1)S(1)} %copy-done.4), kind=kOutput, calls=%fused_computation.42 | convolution fusion | flops 8592031744 | bytes 20971520 | tf_op jit(solution)/shard_map/acnf,ang->cfg/dot_general | solution.py:138
  (108 shorter events, 27.9 us)
Async XLA Ops:
  7.2 86.1 %copy-start = (bf16[512,1024]{1,0:T(8,128)(2,1)S(1)}, bf16[512,1024]{1,0:T(8,128)(2,1)}, u32[]{:S(2)}) copy-start(bf16[512,1024]{1,0:T(8,128)(2,1)} %param.9) | copy-start | bytes 3145732
  7.2 86.1 %copy-start.3 = (s32[6]{0:T(128)S(1)}, s32[6]{0:T(128)}, u32[]{:S(2)}) copy-start(s32[6]{0:T(128)} %param.13) | copy-start | bytes 76
  7.2 86.0 %all-gather.9.cloned.1.call-start = ((), (), s32[]{:S(2)}) async-start(), calls=%async_computation.1 | async-start | bytes 5242880 | tf_op jit(solution)/shard_map/all_gather | solution.py:39
  9.6 165.0 %all-gather.7.cloned.1.call-start = ((), (), s32[]{:S(2)}) async-start(), calls=%async_computation | async-start | bytes 5242880 | tf_op jit(solution)/shard_map/all_gather | solution.py:40
  12.0 243.5 %all-gather.15.cloned.1.call-start = ((), (), s32[]{:S(2)}) async-start(), calls=%async_computation.4 | async-start | bytes 5242880 | tf_op jit(solution)/shard_map/all_gather | solution.py:105
  12.7 324.2 %all-gather.13.cloned.1.call-start = ((), (), s32[]{:S(2)}) async-start(), calls=%async_computation.3 | async-start | bytes 5242880 | tf_op jit(solution)/shard_map/all_gather | solution.py:104
  15.0 447.3 %all-gather.11.cloned.1.call-start = ((), (), s32[]{:S(2)}) async-start(), calls=%async_computation.2 | async-start | bytes 9437184 | tf_op jit(solution)/shard_map/all_gather | solution.py:122
  208.8 128.1 %copy-start.2 = (bf16[512,1024]{1,0:T(8,128)(2,1)S(1)}, bf16[512,1024]{1,0:T(8,128)(2,1)}, u32[]{:S(2)}) copy-start(bf16[512,1024]{1,0:T(8,128)(2,1)} %param.10) | copy-start | bytes 3145732
  212.0 375.6 %all-gather.17.cloned.1.call-start = ((), (), s32[]{:S(2)}) async-start(), calls=%async_computation.5 | async-start | bytes 9437184 | tf_op jit(solution)/shard_map/all_gather | solution.py:123
  352.7 390.6 %all-reduce.3.cloned.1.call-start = ((), (), s32[]{:S(2)}) async-start(), calls=%async_computation.6 | async-start | bytes 16777216 | tf_op jit(solution)/shard_map/psum | solution.py:13
  743.3 14.6 %copy-start.1 = (bf16[2,1024,4,512]{3,1,0,2:T(8,128)(2,1)S(1)}, bf16[2,1024,4,512]{3,1,0,2:T(8,128)(2,1)}, u32[]{:S(2)}) copy-start(bf16[2,1024,4,512]{3,1,0,2:T(8,128)(2,1)} %copy.67) | copy-start | bytes 25165828
  743.3 14.6 %copy-start.4 = (bf16[4,512,1024]{2,1,0:T(8,128)(2,1)S(1)}, bf16[4,512,1024]{2,1,0:T(8,128)(2,1)}, u32[]{:S(2)}) copy-start(bf16[4,512,1024]{2,1,0:T(8,128)(2,1)} %get-tuple-element.384) | copy-start | bytes 12582916
Sparse Core Ops, SparseCore 0:
  9.7 83.4 all-gather.8
  95.4 79.2 all-gather.6
  176.2 79.2 all-gather.14
  256.9 79.9 all-gather.12
  339.5 122.8 all-gather.10
  464.9 122.6 all-gather.16
  592.2 151.0 all-reduce.2
where the time goes:
time: 777 us; the launch traced here: 776 us
  waiting for transfers between devices  594 us (76%)
  matrix products  67.8 us (9%)
  local copies, waits for them, and re-layouts  56 us (7%)
  other arithmetic  22.4 us (3%)
  blocking collectives  15.2 us (2%)
  between operations  14.2 us (2%)
    psum x1, waiting for transfers between devices, spread(): return lax.psum(kept, axis)  128 us
    all_gather x1, waiting for transfers between devices, on_device(): lax.all_gather(value_grads[None], ('tokens', 'cols'), axis=0, tiled=True)  121 us
    all_gather x1, waiting for transfers between devices, on_device(): lax.all_gather(attended[None], ('tokens', 'cols'), axis=0, tiled=True)  109 us
    all_gather x1, waiting for transfers between devices, on_device(): lax.all_gather(key_in, 'tokens', axis=0, tiled=True)  78.1 us
    all_gather x1, waiting for transfers between devices, on_device(): query_rows = lax.all_gather(query_in, 'tokens', axis=0, tiled=True)  59.8 us
    all_gather x1, waiting for transfers between devices, on_device(): lax.all_gather(value_in, 'tokens', axis=0, tiled=True)  54.3 us
    all_gather x1, waiting for transfers between devices, on_device(): grad_rows = lax.all_gather(out_grads, 'tokens', axis=0, tiled=True)  42.4 us
    dot_general x4, matrix products, update(): jnp.einsum('hqk,khd->qhd', weights, value_rows, preferred_element_type=jn...  20.8 us
  transfers between devices with their start and end apart: 7, of which 7 were waited for; matrix products, arithmetic and copies ran while one was open for 15% of the time, Pallas kernels for 0%

commit v1 on v0

--- a/solution.py
+++ b/solution.py
@@ -102,7 +102,17 @@
     attended = weighted.reshape(tok_dev, row_width).astype(jnp.bfloat16)
     stats_all = lax.all_gather(log_total.T, "tokens", axis=0, tiled=True)
     query_rows = lax.all_gather(query_in, "tokens", axis=0, tiled=True)
-    grad_rows = lax.all_gather(out_grads, "tokens", axis=0, tiled=True)
+    dev_count = lax.axis_size("tokens")
+    rack = [out_grads]
+    for u in tuple(range(dev_count - 1)):
+        rack.append(
+            lax.ppermute(
+                rack[-1], "tokens", [(tick, (tick + 1) % dev_count) for tick in range(dev_count)]
+            )
+        )
+    grad_rows = jnp.roll(
+        jnp.concatenate(rack[::-1], 0), (lax.axis_index("tokens") + 1) * out_grads.shape[0], 0
+    )
     piece_rows = query_rows.shape[0]
     piece_pos = jnp.arange(piece_rows, dtype=jnp.int32)
 

time: 777 us -> 745 us (0.959)
  waiting for transfers between devices: 594 us -> 486 us
  starting transfers between devices: 0.51 us -> 28.5 us
  blocking collectives: 15.2 us -> 32.6 us
  matrix products: 67.8 us -> 81.8 us
  other arithmetic: 22.4 us -> 33 us
    ppermute x0 -> x3, waiting for transfers between devices: none -> 123 us  [on_device(): lax.ppermute(rack[-1], 'tokens', [(tick, (tick + 1) % dev_count) for tick...]
    all_gather x1, waiting for transfers between devices: 78.1 us -> 0.01 us  [on_device(): lax.all_gather(key_in, 'tokens', axis=0, tiled=True)]
    all_gather x1, waiting for transfers between devices: 59.8 us -> 0.01 us  [on_device(): query_rows = lax.all_gather(query_in, 'tokens', axis=0, tiled=True)]
    all_gather x1 -> x0, waiting for transfers between devices: 42.4 us -> none  [on_device(): grad_rows = lax.all_gather(out_grads, 'tokens', axis=0, tiled=True)]
    all_gather x1, waiting for transfers between devices: 121 us -> 87.9 us  [on_device(): lax.all_gather(value_grads[None], ('tokens', 'cols'), axis=0, tiled=True)]
    ppermute x0 -> x3, starting transfers between devices: none -> 28 us  [on_device(): lax.ppermute(rack[-1], 'tokens', [(tick, (tick + 1) % dev_count) for tick...]
    all_gather x1, waiting for transfers between devices: 54.3 us -> 26.7 us  [on_device(): lax.all_gather(value_in, 'tokens', axis=0, tiled=True)]
    all_gather x1, blocking collectives: 15.2 us -> 32.6 us  [on_device(): stats_all = lax.all_gather(log_total.T, 'tokens', axis=0, tiled=True)]
  transfers between devices with their start and end apart: 7 -> 9, of which waited for: 7 -> 7; matrix products, arithmetic and copies ran while one was open for 15% -> 19% of each run, Pallas kernels for 0% -> 0%
where the time goes in v1:
time: 745 us; the launch traced here: 744 us
  waiting for transfers between devices  486 us (65%)
  matrix products  81.8 us (11%)
  local copies, waits for them, and re-layouts  61.6 us (8%)
  other arithmetic  33 us (4%)
  blocking collectives  32.6 us (4%)
  starting transfers between devices  28.5 us (4%)
  between operations  14.3 us (2%)
    psum x1, waiting for transfers between devices, spread(): return lax.psum(kept, axis)  128 us
    ppermute x3, waiting for transfers between devices, on_device(): lax.ppermute(rack[-1], 'tokens', [(tick, (tick + 1) % dev_count) for tick...  123 us
    all_gather x1, waiting for transfers between devices, on_device(): lax.all_gather(attended[None], ('tokens', 'cols'), axis=0, tiled=True)  121 us
    all_gather x1, waiting for transfers between devices, on_device(): lax.all_gather(value_grads[None], ('tokens', 'cols'), axis=0, tiled=True)  87.9 us
    all_gather x1, blocking collectives, on_device(): stats_all = lax.all_gather(log_total.T, 'tokens', axis=0, tiled=True)  32.6 us
    ppermute x3, starting transfers between devices, on_device(): lax.ppermute(rack[-1], 'tokens', [(tick, (tick + 1) % dev_count) for tick...  28 us
    all_gather x1, waiting for transfers between devices, on_device(): lax.all_gather(value_in, 'tokens', axis=0, tiled=True)  26.7 us
    dot_general x4, matrix products, update(): jnp.einsum('hqk,khd->qhd', weights, value_rows, preferred_element_type=jn...  21 us
  transfers between devices with their start and end apart: 9, of which 7 were waited for; matrix products, arithmetic and copies ran while one was open for 19% of the time, Pallas kernels for 0%

profile of v1, /device:TPU:0, one launch (start us, length us, event | category | flops | bytes accessed | tf_op | source)
XLA Modules:
  0.0 743.8 jit_solution(13328307158469663013)
XLA Ops:
  15.1 41.5 %collective-permute-done = bf16[512,1024]{1,0:T(8,128)(2,1)S(1)} collective-permute-done((bf16[512,1024]{1,0:T(8,128)(2,1)}, bf16[512,1024]{1,0:T(8,128)(2,1)S(1)}, u32[]{:S(2)}, u32[]{:S(2)}) %collective-permute-start) | collective-permute-done | bytes 1048608 | tf_op jit(solution)/shard_map/ppermute | solution.py:109
  56.6 17.8 %collective-permute-start.1 = (bf16[512,1024]{1,0:T(8,128)(2,1)S(1)}, bf16[512,1024]{1,0:T(8,128)(2,1)S(1)}, u32[]{:S(2)}, u32[]{:S(2)}) collective-permute-start(bf16[512,1024]{1,0:T(8,128)(2,1)S(1)} %collective-permute-done), channel_id=1, source_target_pairs={{0,2},{2,4},{4,6},{6,0},{1,3},{3,5},{5,7},{7,1},{8,10},{10,12},{12... | collective-permute-start | bytes 3145736 | tf_op jit(solution)/shard_map/ppermute | solution.py:109
  76.9 45.2 %collective-permute-done.1 = bf16[512,1024]{1,0:T(8,128)(2,1)S(1)} collective-permute-done((bf16[512,1024]{1,0:T(8,128)(2,1)S(1)}, bf16[512,1024]{1,0:T(8,128)(2,1)S(1)}, u32[]{:S(2)}, u32[]{:S(2)}) %collective-permute-start.1) | collective-permute-done | bytes 1048608 | tf_op jit(solution)/shard_map/ppermute | solution.py:109
  122.1 7.1 collective-permute-start.2
  130.9 36.1 %collective-permute-done.2 = bf16[512,1024]{1,0:T(8,128)(2,1)} collective-permute-done((bf16[512,1024]{1,0:T(8,128)(2,1)S(1)}, bf16[512,1024]{1,0:T(8,128)(2,1)}, u32[]{:S(2)}, u32[]{:S(2)}) %collective-permute-start.2) | collective-permute-done | bytes 1048608 | tf_op jit(solution)/shard_map/ppermute | solution.py:109
  172.5 6.4 copy.62
  178.9 50.3 %while.30 = (s32[]{:T(128)}, f32[8,512]{1,0:T(8,128)S(1)}, f32[8,512]{1,0:T(8,128)S(1)}, s32[6]{0:T(128)S(1)}, s32[4]{0:T(128)S(1)}, /*index=5*/bf16[2048,1024]{...) while((s32[]{:T(128)}, f32[8,512]{1,0:T(8,128)S(1)}, ...), condition=%wide.region_5.6_spmd.clone, body=%wide.region_0.5_spmd.clone.sunk | while | flops 553950208 | bytes 21995740 | solution.py:75
  181.9 5.1 fusion.59
  187.0 4.5 select_reduce_fusion.2
  194.5 5.1 fusion.59
  199.6 4.5 select_reduce_fusion.2
  207.1 5.1 fusion.59
  212.2 4.5 select_reduce_fusion.2
  219.6 5.1 fusion.59
  224.8 4.5 select_reduce_fusion.2
  229.3 32.6 %all_gather.22 = f32[2048,8]{0,1:T(8,128)S(1)} all-gather(f32[512,8]{0,1:T(8,128)S(1)} %bitcast.132), channel_id=1, replica_groups=mesh['heads'=4,'tokens'=4,'cols'=2] {'tokens'}, dimensions={0}, use_global_device_ids=true | all-gather | bytes 81920 | tf_op jit(solution)/shard_map/all_gather | solution.py:103
  261.9 14.7 %fusion.29 = bf16[8,128,512]{2,1,0:T(8,128)(2,1)S(1)} fusion(bf16[2048,8,128]{0,2,1:T(8,128)(2,1)} %bitcast.130, bf16[2048,8,128]{0,2,1:T(8,128)(2,1)} %bitcast.134, f32[8,2048]{1,0:T(8,128)S(1)} %bitcast.133, pred[2048,512]{1,0:T(8,128)(4,1)} %broadcast_compare_fusion.2, bf16[512,1024]{1,0:T(8,128)(2,1)S(1)} %copy-done.3), kind=kOutput, calls=%fused_computation.50 | convolution fusion | flops 4329046016 | bytes 11599872 | tf_op jit(solution)/shard_map/hqk,qhd->khd/dot_general | solution.py:125
  278.0 26.7 %all-gather.6.cloned.1.call-done = bf16[2048,1024]{0,1:T(8,128)(2,1)} async-done(((bf16[512,1024]{0,1:T(8,128)(2,1)}), bf16[2048,1024]{0,1:T(8,128)(2,1)}) %all-gather.6.cloned.1.call-update) | async-done | bytes 4194320 | tf_op jit(solution)/shard_map/all_gather | solution.py:40
  304.7 34.5 %while.31 = (s32[]{:T(128)}, f32[512,8,128]{0,2,1:T(8,128)}, s32[4]{0:T(128)S(1)}, bf16[2048,1024]{0,1:T(8,128)(2,1)}, s32[6]{0:T(128)S(1)}, /*index=5*/bf16[204...) while((s32[]{:T(128)}, f32[512,8,128]{0,2,1:T(8,128)}, ...), condition=%wide.region_9.10_spmd.clone, body=%wide.region_6.9_spmd.clone.sunk | while | flops 1083460608 | bytes 12099813 | solution.py:101
  308.0 4.0 bitcast_add_fusion.2
  315.6 5.7 bitcast_add_fusion.2
  324.6 5.6 bitcast_add_fusion.2
  333.5 5.6 bitcast_add_fusion.2
  342.5 87.9 %all-gather.14.cloned.1.call-done = bf16[8,512,1024]{2,1,0:T(8,128)(2,1)} async-done(((bf16[1,512,1024]{2,1,0:T(8,128)(2,1)}), bf16[8,512,1024]{2,1,0:T(8,128)(2,1)}) %all-gather.14.cloned.1.call-update) | async-done | bytes 8388624 | tf_op jit(solution)/shard_map/all_gather | solution.py:133
  430.4 4.5 fusion.26
  434.9 120.7 %all-gather.10.cloned.1.call-done = bf16[8,512,1024]{2,1,0:T(8,128)(2,1)} async-done(((bf16[1,512,1024]{2,1,0:T(8,128)(2,1)}), bf16[8,512,1024]{2,1,0:T(8,128)(2,1)}) %all-gather.10.cloned.1.call-update) | async-done | bytes 8388624 | tf_op jit(solution)/shard_map/all_gather | solution.py:132
  555.6 4.5 fusion.27
  560.1 11.6 %copy.67 = bf16[2,1024,4,512]{3,1,0,2:T(8,128)(2,1)} copy(bf16[2,1024,4,512]{1,3,0,2:T(8,128)(2,1)} %bitcast.124) | data formatting | bytes 16777216 | tf_op jit(solution)/shard_map/acnf,ang->cfg/dot_general | solution.py:148
  571.7 11.4 %copy.60 = bf16[2,1024,4,512]{3,1,0,2:T(8,128)(2,1)} copy(bf16[2,1024,4,512]{1,3,0,2:T(8,128)(2,1)} %bitcast.126) | data formatting | bytes 16777216 | tf_op jit(solution)/shard_map/acnf,ang->cfg/dot_general | solution.py:145
  583.1 128.2 %all-reduce.3.cloned.1.call-done = (bf16[4,512,1024]{2,1,0:T(8,128)(2,1)}, bf16[4,512,1024]{2,1,0:T(8,128)(2,1)}) async-done(((bf16[4,512,1024]{2,1,0:T(8,128)(2,1)}, bf16[4,512,1024]{2,1,0:T(8,128)(2,1)}), (bf16[4,512,1024]{2,1,0:T(8,128)(2,1)}, bf16[4,512,1024]{2,1,0:T(8,128)(2,1)})) %all-reduce.3.cloned.1.call-update) | async-done | bytes 8388624 | tf_op jit(solution)/shard_map/psum | solution.py:13
  711.4 14.6 %bitcast_multiply_fusion = f32[2048,1024]{1,0:T(8,128)} fusion(bf16[2048,4,512]{2,0,1:T(8,128)(2,1)} %bitcast.128, bf16[4,512,1024]{2,1,0:T(8,128)(2,1)} %get-tuple-element.384), kind=kOutput, calls=%fused_computation.42 | convolution fusion | flops 8592031744 | bytes 20971520 | tf_op jit(solution)/shard_map/acnf,ang->cfg/dot_general | solution.py:148
  726.0 11.0 %bitcast_multiply_fusion.1 = f32[2048,1024]{1,0:T(8,128)} fusion(bf16[2048,4,512]{2,0,1:T(8,128)(2,1)S(1)} %bitcast.127, bf16[4,512,1024]{2,1,0:T(8,128)(2,1)S(1)} %copy-done.5), kind=kOutput, calls=%fused_computation.43 | convolution fusion | flops 8592031744 | bytes 20971520 | tf_op jit(solution)/shard_map/acnf,ang->cfg/dot_general | solution.py:145
  (122 shorter events, 42.0 us)
Async XLA Ops:
  7.2 161.2 %copy-start.2 = (bf16[512,1024]{1,0:T(8,128)(2,1)S(1)}, bf16[512,1024]{1,0:T(8,128)(2,1)}, u32[]{:S(2)}) copy-start(bf16[512,1024]{1,0:T(8,128)(2,1)} %param.12) | copy-start | bytes 3145732
  7.2 69.7 %copy-start.4 = (s32[6]{0:T(128)S(1)}, s32[6]{0:T(128)}, u32[]{:S(2)}) copy-start(s32[6]{0:T(128)} %param.13) | copy-start | bytes 76
  7.2 171.7 %all-gather.8.cloned.1.call-start = ((), (), s32[]{:S(2)}) async-start(), calls=%async_computation.1 | async-start | bytes 5242880 | tf_op jit(solution)/shard_map/all_gather | solution.py:39
  9.6 252.3 %all-gather.12.cloned.1.call-start = ((), (), s32[]{:S(2)}) async-start(), calls=%async_computation.3 | async-start | bytes 5242880 | tf_op jit(solution)/shard_map/all_gather | solution.py:104
  12.0 292.7 %all-gather.6.cloned.1.call-start = ((), (), s32[]{:S(2)}) async-start(), calls=%async_computation | async-start | bytes 5242880 | tf_op jit(solution)/shard_map/all_gather | solution.py:40
  12.0 44.6 %collective-permute-start = (bf16[512,1024]{1,0:T(8,128)(2,1)}, bf16[512,1024]{1,0:T(8,128)(2,1)S(1)}, u32[]{:S(2)}, u32[]{:S(2)}) collective-permute-start(bf16[512,1024]{1,0:T(8,128)(2,1)} %param.12), channel_id=1, source_target_pairs={{0,2},{2,4},{4,6},{6,0},{1,3},{3,5},{5,7},{7,1},{8,10},{10,12},{12... | collective-permute-start | bytes 3145736 | tf_op jit(solution)/shard_map/ppermute | solution.py:109
  56.6 65.5 %collective-permute-start.1 = (bf16[512,1024]{1,0:T(8,128)(2,1)S(1)}, bf16[512,1024]{1,0:T(8,128)(2,1)S(1)}, u32[]{:S(2)}, u32[]{:S(2)}) collective-permute-start(bf16[512,1024]{1,0:T(8,128)(2,1)S(1)} %collective-permute-done), channel_id=1, source_target_pairs={{0,2},{2,4},{4,6},{6,0},{1,3},{3,5},{5,7},{7,1},{8,10},{10,12},{12... | collective-permute-start | bytes 3145736 | tf_op jit(solution)/shard_map/ppermute | solution.py:109
  76.8 353.6 %all-gather.14.cloned.1.call-start = ((), (), s32[]{:S(2)}) async-start(), calls=%async_computation.4 | async-start | bytes 9437184 | tf_op jit(solution)/shard_map/all_gather | solution.py:133
  122.1 44.8 %collective-permute-start.2 = (bf16[512,1024]{1,0:T(8,128)(2,1)S(1)}, bf16[512,1024]{1,0:T(8,128)(2,1)}, u32[]{:S(2)}, u32[]{:S(2)}) collective-permute-start(bf16[512,1024]{1,0:T(8,128)(2,1)S(1)} %collective-permute-done.1), channel_id=1, source_target_pairs={{0,2},{2,4},{4,6},{6,0},{1,3},{3,5},{5,7},{7,1},{8,10},{10,12},{12... | collective-permute-start | bytes 3145736 | tf_op jit(solution)/shard_map/ppermute | solution.py:109
  170.0 8.9 %copy-start = (bf16[512,1024]{1,0:T(8,128)(2,1)S(1)}, bf16[512,1024]{1,0:T(8,128)(2,1)}, u32[]{:S(2)}) copy-start(bf16[512,1024]{1,0:T(8,128)(2,1)} %param.9) | copy-start | bytes 3145732
  178.9 83.0 %copy-start.3 = (bf16[512,1024]{1,0:T(8,128)(2,1)S(1)}, bf16[512,1024]{1,0:T(8,128)(2,1)}, u32[]{:S(2)}) copy-start(bf16[512,1024]{1,0:T(8,128)(2,1)} %param.10) | copy-start | bytes 3145732
  277.9 277.7 %all-gather.10.cloned.1.call-start = ((), (), s32[]{:S(2)}) async-start(), calls=%async_computation.2 | async-start | bytes 9437184 | tf_op jit(solution)/shard_map/all_gather | solution.py:132
  342.3 369.1 %all-reduce.3.cloned.1.call-start = ((), (), s32[]{:S(2)}) async-start(), calls=%async_computation.5 | async-start | bytes 16777216 | tf_op jit(solution)/shard_map/psum | solution.py:13
  711.4 14.6 %copy-start.1 = (bf16[2,1024,4,512]{3,1,0,2:T(8,128)(2,1)S(1)}, bf16[2,1024,4,512]{3,1,0,2:T(8,128)(2,1)}, u32[]{:S(2)}) copy-start(bf16[2,1024,4,512]{3,1,0,2:T(8,128)(2,1)} %copy.60) | copy-start | bytes 25165828
  711.4 14.6 %copy-start.5 = (bf16[4,512,1024]{2,1,0:T(8,128)(2,1)S(1)}, bf16[4,512,1024]{2,1,0:T(8,128)(2,1)}, u32[]{:S(2)}) copy-start(bf16[4,512,1024]{2,1,0:T(8,128)(2,1)} %get-tuple-element.383) | copy-start | bytes 12582916
Sparse Core Ops, SparseCore 0:
  9.7 121.1 all-gather.7
  132.5 89.9 all-gather.11
  224.0 80.5 all-gather.5
  307.2 123.1 all-gather.13
  432.9 122.6 all-gather.9
  560.2 151.0 all-reduce.2
